TPU v7x, 16 devices: a whole 2x2x2 slice. The times are simulated.
16 devices in a mesh: data: 4 (over z, y), tp: 4 (over x, core).
Axes of the slice: x: 2, y: 2, z: 2, core: 2. Of those that a mesh axis runs over, the one named last changes fastest.
Arguments:
- x: bfloat16 [1024, 32768], P('data', 'tp'), parts along dimension 0
- w: bfloat16 [32768, 8192], P('tp')
- lengths: int32 [16], P('data'), parts along dimension 0
Outputs:
- output: bfloat16 [1024, 8192], P('data'), parts along dimension 0
There are 4 independent parts. A program takes and returns all parts, laid end to end along the dimension named above; an argument that names none is the same for every part.
All inputs are finite; a program needn't handle non-finite values.
Results may differ from a plain program's by a relative error of at most 0.001.
Values are sent between devices in bfloat16 or wider.
A program may use at most 1 GiB of HBM per device.

v0:
```python
import jax
import jax.numpy as jnp
from jax import lax
from jax.sharding import PartitionSpec as P


def solution(mesh):
    tp_size = mesh.shape["tp"]

    def local_part(x_loc, w_loc, lengths):
        tokens = x_loc.shape[0]
        seq_len = tokens // lengths.shape[0]
        rows_dev = tokens // tp_size
        part_sum = jnp.dot(x_loc, w_loc, preferred_element_type=jnp.float32)
        own_rows = lax.psum_scatter(part_sum, "tp", scatter_dimension=0, tiled=True)
        valid = (jnp.arange(seq_len, dtype=jnp.int32)[None, :] < lengths[:, None]).reshape(-1)
        own_valid = lax.dynamic_slice_in_dim(valid, lax.axis_index("tp") * rows_dev, rows_dev)
        own_out = jnp.where(own_valid[:, None], own_rows, 0.0).astype(jnp.bfloat16)
        return lax.all_gather(own_out, "tp", axis=0, tiled=True)

    return jax.shard_map(local_part, mesh=mesh, in_specs=(P("data", "tp"), P("tp", None), P("data")), out_specs=P("data", None), check_vma=False)
```

profile of v0, /device:TPU:0, one launch (start us, length us, event | category | flops | bytes accessed | tf_op | source)
XLA Modules:
  0.0 177.1 jit_solution(2182769150886955337)
XLA Ops:
  6.5 0.0 reduce-scatter.2.cloned.1.call-start
  6.5 53.8 %fusion = f32[256,8192]{1,0:T(8,128)} fusion(bf16[256,8192]{1,0:T(8,128)(2,1)} %param.3, bf16[8192,8192]{1,0:T(8,128)(2,1)} %param.4), kind=kOutput, calls=%fused_computation.2 | convolution fusion | flops 34359738368 | bytes 146800640 | tf_op jit(solution)/shard_map/dot_general | solution.py:14
  60.3 0.0 copy-start
  60.4 0.0 reduce-scatter.2.cloned.1.call-update
  60.4 0.0 all-gather.2.cloned.1.call-start
  60.4 0.6 copy-done
  61.0 0.1 iota_compare_fusion
  61.1 0.1 lt.23
  61.2 0.1 dynamic_slice.3
  61.2 69.0 %reduce-scatter.2.cloned.1.call-done = f32[64,8192]{1,0:T(8,128)} async-done(((f32[256,8192]{1,0:T(8,128)}), f32[64,8192]{1,0:T(8,128)}) %reduce-scatter.2.cloned.1.call-update) | async-done | bytes 2097168 | tf_op jit(solution)/shard_map/reduce_scatter | solution.py:15
  130.3 2.7 %select_convert_fusion = bf16[64,8192]{1,0:T(8,128)(2,1)} fusion(f32[64,8192]{1,0:T(8,128)} %reduce-scatter.2.cloned.1.call-done, pred[64]{0:T(512)(128)(4,1)S(1)} %dynamic_slice.3), kind=kLoop, calls=%fused_computation | loop fusion | flops 524288 | bytes 3145792 | tf_op jit(solution)/shard_map/convert_element_type | solution.py:18
  133.0 0.0 all-gather.2.cloned.1.call-update
  133.0 32.6 %all-gather.2.cloned.1.call-done = bf16[256,8192]{1,0:T(8,128)(2,1)} async-done(((bf16[64,8192]{1,0:T(8,128)(2,1)}), bf16[256,8192]{1,0:T(8,128)(2,1)}) %all-gather.2.cloned.1.call-update) | async-done | bytes 4194320 | tf_op jit(solution)/shard_map/all_gather | solution.py:19
  165.6 4.6 %copy.5 = bf16[256,8192]{1,0:T(8,128)(2,1)} copy(bf16[256,8192]{1,0:T(8,128)(2,1)} %all-gather.2.cloned.1.call-done) | data formatting | bytes 8388608
Async XLA Ops:
  6.5 123.7 %reduce-scatter.2.cloned.1.call-start = ((), (), s32[]{:S(2)}) async-start(), calls=%async_computation.1 | async-start | bytes 10485760 | tf_op jit(solution)/shard_map/reduce_scatter | solution.py:15
  60.3 0.7 copy-start
  60.4 105.2 %all-gather.2.cloned.1.call-start = ((), (), s32[]{:S(2)}) async-start(), calls=%async_computation.2 | async-start | bytes 5242880 | tf_op jit(solution)/shard_map/all_gather | solution.py:19
Sparse Core Ops, SparseCore 0:
  60.5 69.7 reduce-scatter.1
  133.2 32.4 all-gather.1
where the time goes:
time: 177 us
  waiting for transfers between devices  102 us (58%)
  matrix products  53.8 us (30%)
  between operations  13.4 us (8%)
  local copies, waits for them, and re-layouts  5.38 us (3%)
  other arithmetic  2.82 us (2%)
    reduce_scatter x1, waiting for transfers between devices, local_part(): own_rows = lax.psum_scatter(part_sum, 'tp', scatter_dimension=0, tiled=True)  69 us
    dot_general x1, matrix products, local_part(): part_sum = jnp.dot(x_loc, w_loc, preferred_element_type=jnp.float32)  53.8 us
    all_gather x1, waiting for transfers between devices, local_part(): return lax.all_gather(own_out, 'tp', axis=0, tiled=True)  32.6 us
    unnamed x3, local copies, waits for them, and re-layouts  5.21 us
  transfers between devices with their start and end apart: 2, of which 2 were waited for; matrix products, arithmetic and copies ran while one was open for 0% of the time, Pallas kernels for 0%

commit v1 on v0

v1 whole, which is shorter than its diff:
```python
import functools

import jax
import jax.numpy as jnp
from jax import lax
from jax.experimental import pallas as pl
from jax.experimental.pallas import tpu as pltpu
from jax.sharding import PartitionSpec as P

MESH = pl.DeviceIdType.MESH
ROWS = 208
CN = 512
KB = 2048
SLOTS = 8
LAG_B, LAG_C, LAG_D = 1, 3, 5


def row_targets(len_ref, shape, axis, seq_len):
    row = lax.broadcasted_iota(jnp.int32, shape, axis)
    target = jnp.full(shape, -1, jnp.int32)
    start = jnp.int32(0)
    for s in range(len_ref.shape[0]):
        inside = (row >= s * seq_len) & (row < s * seq_len + len_ref[s])
        target = jnp.where(inside, row - s * seq_len + start, target)
        start = start + len_ref[s]
    return target


def matmul_kernel(len_ref, x_hbm, w_hbm, y_ref, x_buf, xc, w_buf, part, d2d_in, ici_in,
                  x_sem, w_sem, d2d_s, d2d_r, ici_s, ici_r, yx_s, yx_r, yp_s, yp_r, yf_s, yf_r):
    tokens, depth = x_hbm.shape
    rows = xc.shape[0]
    width = w_hbm.shape[1]
    nc, nk = width // CN, depth // KB
    total = nc * nk
    seq_len = tokens // len_ref.shape[0]
    tp = lax.axis_index("tp")
    me_x, me_c = tp // 2, lax.rem(tp, 2)
    nbr = {"tp": (1 - me_x) * 2 + me_c}
    partner = {"tp": me_x * 2 + (1 - me_c)}

    def w_copy(t, slot):
        j, k = t // nk, lax.rem(t, nk)
        return pltpu.make_async_copy(
            w_hbm.at[pl.ds(pl.multiple_of(k * KB, KB), KB), pl.ds(pl.multiple_of(j * CN, CN), CN)],
            w_buf.at[slot], w_sem.at[slot])

    def x_copy(k):
        cols = pl.ds(k * KB, KB)
        return pltpu.make_async_copy(x_hbm.at[:, cols], x_buf.at[:, cols], x_sem.at[k])

    for k in range(nk):
        x_copy(k).start()
    for t in range(SLOTS):
        w_copy(t, t).start()

    barrier = pltpu.get_barrier_semaphore()
    for dev in (partner, nbr):
        pl.semaphore_signal(barrier, inc=1, device_id=dev, device_id_type=MESH)

    pos = lax.broadcasted_iota(jnp.int32, (rows, tokens), 0)
    pick = (pos == row_targets(len_ref, (rows, tokens), 1, seq_len)).astype(jnp.bfloat16)
    for k in range(nk):
        x_copy(k).wait()

        @pl.loop(0, KB // 512)
        def _(i):
            cols = pl.ds(pl.multiple_of(k * KB + i * 512, 512), 512)
            xc[:, cols] = jnp.dot(pick, x_buf[:, cols], preferred_element_type=jnp.float32).astype(jnp.bfloat16)

    pl.semaphore_wait(barrier, 2)

    def remote(src, dst, s, r, dev):
        return pltpu.make_async_remote_copy(src_ref=src, dst_ref=dst, send_sem=s, recv_sem=r,
                                            device_id=dev, device_id_type=MESH)

    def d2d_copy(j):
        return remote(part.at[j, 1 - me_c], d2d_in.at[j], d2d_s.at[j], d2d_r.at[j], partner)

    def ici_copy(j):
        return remote(d2d_in.at[j, 1 - me_x], ici_in.at[j], ici_s.at[j], ici_r.at[j], nbr)

    def yx_copy(j):
        q = y_ref.at[j, me_c, me_x]
        return remote(q, q, yx_s.at[j], yx_r.at[j], nbr)

    def yp_copy(j):
        q = y_ref.at[j, me_c, me_x]
        return remote(q, q, yp_s.at[j], yp_r.at[j], partner)

    def yf_copy(j):
        q = y_ref.at[j, me_c, 1 - me_x]
        return remote(q, q, yf_s.at[j], yf_r.at[j], partner)

    def stage_a(j):
        d2d_copy(j).start()

    def stage_b(j):
        d2d_copy(j).wait_recv()
        d2d_in[j, 1 - me_x] = d2d_in[j, 1 - me_x] + part[j, me_c, 1 - me_x]
        d2d_in[j, me_x] = d2d_in[j, me_x] + part[j, me_c, me_x]
        ici_copy(j).start()

    def stage_c(j):
        ici_copy(j).wait_recv()
        y_ref[j, me_c, me_x] = (d2d_in[j, me_x] + ici_in[j]).astype(jnp.bfloat16)
        yx_copy(j).start()
        yp_copy(j).start()

    def stage_d(j):
        yx_copy(j).wait_recv()
        yf_copy(j).start()

    stages = ((stage_b, LAG_B), (stage_c, LAG_C), (stage_d, LAG_D))

    @pl.loop(0, nc)
    def _(j):
        for k in range(nk):
            t = j * nk + k
            slot = lax.rem(t, SLOTS)
            w_copy(t, slot).wait()
            got = jnp.dot(xc[:, k * KB:(k + 1) * KB], w_buf[slot], preferred_element_type=jnp.float32)
            for q in range(4):
                piece = got[:, q * 128:(q + 1) * 128]
                if k:
                    part[j, q // 2, q % 2] += piece
                else:
                    part[j, q // 2, q % 2] = piece

            @pl.when(t + SLOTS < total)
            def _():
                w_copy(t + SLOTS, slot).start()

            if 0 < k <= len(stages):
                stage, lag = stages[k - 1]

                @pl.when(j >= lag)
                def _():
                    stage(j - lag)
        stage_a(j)

    for step in range(nc, nc + LAG_D):
        for stage, lag in stages:
            if step - lag < nc:
                stage(step - lag)

    @pl.loop(0, nc)
    def _(j):
        yp_copy(j).wait_recv()
        yf_copy(j).wait_recv()
        d2d_copy(j).wait_send()
        ici_copy(j).wait_send()
        yx_copy(j).wait_send()
        yp_copy(j).wait_send()
        yf_copy(j).wait_send()


def expand_kernel(len_ref, y_ref, out_ref):
    tokens = out_ref.shape[0]
    rows = y_ref.shape[3]
    seq_len = tokens // len_ref.shape[0]
    pos = lax.broadcasted_iota(jnp.int32, (tokens, rows), 1)
    place = (pos == row_targets(len_ref, (tokens, rows), 0, seq_len)).astype(jnp.bfloat16)
    for i in range(y_ref.shape[0]):
        for q in range(4):
            c = (i * 4 + q) * 128
            out_ref[:, c:c + 128] = jnp.dot(place, y_ref[i, q // 2, q % 2], preferred_element_type=jnp.float32).astype(jnp.bfloat16)


def solution(mesh):
    def local_part(x_loc, w_loc, lengths):
        tokens, depth = x_loc.shape
        width = w_loc.shape[1]
        rows, nc, nk = ROWS, width // CN, depth // KB
        dma = lambda n: pltpu.SemaphoreType.DMA((n,))
        y = pl.pallas_call(
            matmul_kernel,
            out_shape=jax.ShapeDtypeStruct((nc, 2, 2, rows, 128), jnp.bfloat16),
            in_specs=[pl.BlockSpec(memory_space=pltpu.SMEM), pl.BlockSpec(memory_space=pl.ANY), pl.BlockSpec(memory_space=pl.ANY)],
            out_specs=pl.BlockSpec(memory_space=pltpu.VMEM),
            scratch_shapes=[
                pltpu.VMEM((tokens, depth), jnp.bfloat16),
                pltpu.VMEM((rows, depth), jnp.bfloat16),
                pltpu.VMEM((SLOTS, KB, CN), jnp.bfloat16),
                pltpu.VMEM((nc, 2, 2, rows, 128), jnp.float32),
                pltpu.VMEM((nc, 2, rows, 128), jnp.float32),
                pltpu.VMEM((nc, rows, 128), jnp.float32),
                dma(nk), dma(SLOTS)] + [dma(nc)] * 10,
            compiler_params=pltpu.CompilerParams(collective_id=0, has_side_effects=True, vmem_limit_bytes=56 * 2**20),
            cost_estimate=pl.CostEstimate(flops=2 * rows * depth * width, bytes_accessed=2 * depth * width, transcendentals=0),
        )(lengths, x_loc, w_loc)
        step = 2
        return pl.pallas_call(
            expand_kernel,
            out_shape=jax.ShapeDtypeStruct((tokens, width), jnp.bfloat16),
            grid=(nc // step,),
            in_specs=[pl.BlockSpec(memory_space=pltpu.SMEM), pl.BlockSpec((step, 2, 2, rows, 128), lambda i: (i, 0, 0, 0, 0))],
            out_specs=pl.BlockSpec((tokens, step * CN), lambda i: (0, i)),
            cost_estimate=pl.CostEstimate(flops=2 * rows * tokens * width, bytes_accessed=4 * tokens * width, transcendentals=0),
        )(lengths, y)

    return jax.shard_map(local_part, mesh=mesh, in_specs=(P("data", "tp"), P("tp", None), P("data")), out_specs=P("data", None), check_vma=False)
```

time: 177 us -> 83 us (0.47)
  waiting for transfers between devices: 102 us -> 0 us
  Pallas kernels: 0 us -> 82.8 us
  matrix products: 53.8 us -> 0 us
  between operations: 13.4 us -> 0.01 us
  local copies, waits for them, and re-layouts: 5.38 us -> 0 us
  other arithmetic: 2.82 us -> 0 us
    pallas_call x0 -> x2, Pallas kernels: none -> 82.8 us  [the longest x1 74.9 us: local_part(): pl.pallas_call(matmul_kernel, out_shape=jax.ShapeDtypeStruct((nc, 2, 2, r...]
    reduce_scatter x1 -> x0, waiting for transfers between devices: 69 us -> none  [local_part(): own_rows = lax.psum_scatter(part_sum, 'tp', scatter_dimension=0, tiled=True)]
    dot_general x1 -> x0, matrix products: 53.8 us -> none  [local_part(): part_sum = jnp.dot(x_loc, w_loc, preferred_element_type=jnp.float32)]
    all_gather x1 -> x0, waiting for transfers between devices: 32.6 us -> none  [local_part(): return lax.all_gather(own_out, 'tp', axis=0, tiled=True)]
    unnamed x3 -> x0, local copies, waits for them, and re-layouts: 5.21 us -> none
    convert_element_type x1 -> x0, other arithmetic: 2.75 us -> none  [local_part(): own_out = jnp.where(own_valid[:, None], own_rows, 0.0).astype(jnp.bfloat16)]
  transfers between devices with their start and end apart: 2 -> 0, of which waited for: 2 -> 0; matrix products, arithmetic and copies ran while one was open for 0% -> 0% of each run, Pallas kernels for 0% -> 0%
where the time goes in v1:
time: 83 us; the launch traced here: 82.8 us
  Pallas kernels  82.8 us (100%)
    pallas_call x1, Pallas kernels, local_part(): pl.pallas_call(matmul_kernel, out_shape=jax.ShapeDtypeStruct((nc, 2, 2, r...  74.9 us
    pallas_call x1, Pallas kernels, local_part(): pl.pallas_call(expand_kernel, out_shape=jax.ShapeDtypeStruct((tokens, wid...  7.91 us

profile of v1, /device:TPU:0, one launch (start us, length us, event | category | flops | bytes accessed | tf_op | source)
XLA Modules:
  0.0 82.8 jit_solution(1702168644960133900)
XLA Ops:
  0.0 74.9 %shard_map.37.y_ref = bf16[16,2,2,208,128]{4,3,2,1,0:T(8,128)(2,1)} custom-call(s32[4]{0:T(128)} %len_ref.3, bf16[256,8192]{1,0:T(8,128)(2,1)} %x_hbm.1, bf16[8192,8192]{1,0:T(8,128)(2,1)} %w_hbm.1), custom_call_target="tpu_custom_call" | custom-call | flops 27917287424 | bytes 134217728 | tf_op jit(solution)/shard_map/pallas_call | solution.py:176
  74.9 7.9 %shard_map.38 = bf16[256,8192]{1,0:T(8,128)(2,1)} custom-call(s32[4]{0:T(128)} %len_ref.3, bf16[16,2,2,208,128]{4,3,2,1,0:T(8,128)(2,1)} %shard_map.37.y_ref), custom_call_target="tpu_custom_call" | custom-call | flops 872415232 | bytes 8388608 | tf_op jit(solution)/shard_map/pallas_call | solution.py:193

commit v2 on v1

v2 whole, which is shorter than its diff:
```python
import functools

import jax
import jax.numpy as jnp
from jax import lax
from jax.experimental import pallas as pl
from jax.experimental.pallas import tpu as pltpu
from jax.sharding import PartitionSpec as P

MESH = pl.DeviceIdType.MESH
CAPS = (128, 144, 160, 176, 192, 208)
CN = 512
KB = 4096
SLOTS = 6
FIRST = 1
LAG_B, LAG_C, LAG_D = 1, 3, 5
RING = 8


def row_targets(len_ref, shape, axis, seq_len):
    row = lax.broadcasted_iota(jnp.int32, shape, axis)
    target = jnp.full(shape, -1, jnp.int32)
    start = jnp.int32(0)
    for s in range(len_ref.shape[0]):
        inside = (row >= s * seq_len) & (row < s * seq_len + len_ref[s])
        target = jnp.where(inside, row - s * seq_len + start, target)
        start = start + len_ref[s]
    return target


def head_kernel(len_ref, x_hbm, w_hbm, pick_ref, xc_out, part_out, x_buf, xc, w_buf, part, mine, theirs,
                x_sem, w_sem, o_sem, p_sem, send, recv):
    tokens, depth = x_hbm.shape
    rows = xc.shape[0]
    nk = depth // KB
    seq_len = tokens // len_ref.shape[0]
    groups = theirs.shape[0] + 1
    me = lax.axis_index("data")
    peers = [{"data": lax.rem(me + r, groups)} for r in range(1, groups)]

    def x_copy(k):
        cols = pl.ds(k * KB, KB)
        return pltpu.make_async_copy(x_hbm.at[:, cols], x_buf.at[:, cols], x_sem.at[k])

    def w_copy(t):
        j, k = t // nk, t % nk
        return pltpu.make_async_copy(w_hbm.at[pl.ds(k * KB, KB), pl.ds(j * CN, CN)], w_buf.at[t], w_sem.at[t])

    def xc_copy(k):
        cols = pl.ds(k * KB, KB)
        return pltpu.make_async_copy(xc.at[:, cols], xc_out.at[:, cols], o_sem.at[k])

    def tell(r):
        return pltpu.make_async_remote_copy(src_ref=mine, dst_ref=theirs.at[r], send_sem=send.at[r], recv_sem=recv.at[r],
                                            device_id=peers[r], device_id_type=MESH)

    for k in range(nk):
        x_copy(k).start()
    for t in range(FIRST * nk):
        w_copy(t).start()
    barrier = pltpu.get_barrier_semaphore()
    for dev in peers:
        pl.semaphore_signal(barrier, inc=1, device_id=dev, device_id_type=MESH)
    total = len_ref[0]
    for s in range(1, len_ref.shape[0]):
        total = total + len_ref[s]
    mine[...] = jnp.full(mine.shape, total, jnp.int32)

    pos = lax.broadcasted_iota(jnp.int32, (rows, tokens), 0)
    pick = (pos == row_targets(len_ref, (rows, tokens), 1, seq_len)).astype(jnp.bfloat16)
    pl.semaphore_wait(barrier, groups - 1)
    for r in range(groups - 1):
        tell(r).start()
    for k in range(nk):
        x_copy(k).wait()

        @pl.loop(0, KB // 1024)
        def _(i):
            cols = pl.ds(pl.multiple_of(k * KB + i * 1024, 1024), 1024)
            xc[:, cols] = jnp.dot(pick, x_buf[:, cols], preferred_element_type=jnp.float32).astype(jnp.bfloat16)

    for t in range(FIRST * nk):
        j, k = t // nk, t % nk
        w_copy(t).wait()
        got = jnp.dot(xc[:, k * KB:(k + 1) * KB], w_buf[t], preferred_element_type=jnp.float32)
        for q in range(4):
            piece = got[:, q * 128:(q + 1) * 128]
            part[j, q // 2, q % 2] = part[j, q // 2, q % 2] + piece if k else piece
        if t == 0:
            for i in range(nk):
                xc_copy(i).start()

    p_copy = pltpu.make_async_copy(part, part_out, p_sem)
    p_copy.start()
    most = mine[...]
    for r in range(groups - 1):
        tell(r).wait()
        most = jnp.maximum(most, theirs[r])
    most = jnp.max(most)
    index = jnp.int32(0)
    for cap in CAPS[:-1]:
        index = index + (most > cap).astype(jnp.int32)
    pick_ref[0] = index
    for k in range(nk):
        xc_copy(k).wait()
    p_copy.wait()


def main_kernel(xc_hbm, part_hbm, w_hbm, y_out, xc, w_buf, part, d2d_in, ici_in, own, other,
                x_sem, p_sem, w_sem, d2d_s, d2d_r, ici_s, ici_r, yx_s, yx_r, yp_s, yp_r, yf_s, yf_r, yl_s, yo_s):
    rows, depth = xc.shape
    width = w_hbm.shape[1]
    nc, nk = width // CN, depth // KB
    total = nc * nk
    tp = lax.axis_index("tp")
    me_x, me_c = tp // 2, lax.rem(tp, 2)
    nbr = {"tp": (1 - me_x) * 2 + me_c}
    partner = {"tp": me_x * 2 + (1 - me_c)}

    def w_copy(t, slot):
        j, k = t // nk, lax.rem(t, nk)
        return pltpu.make_async_copy(
            w_hbm.at[pl.ds(pl.multiple_of(k * KB, KB), KB), pl.ds(pl.multiple_of(j * CN, CN), CN)],
            w_buf.at[slot], w_sem.at[slot])

    def x_copy(k):
        cols = pl.ds(k * KB, KB)
        return pltpu.make_async_copy(xc_hbm.at[pl.ds(0, rows), cols], xc.at[:, cols], x_sem.at[k])

    p_copy = pltpu.make_async_copy(part_hbm.at[:, :, :, pl.ds(0, rows)], part.at[pl.ds(0, FIRST)], p_sem)

    barrier = pltpu.get_barrier_semaphore()
    for dev in (partner, nbr):
        pl.semaphore_signal(barrier, inc=1, device_id=dev, device_id_type=MESH)
    p_copy.start()
    for k in range(nk):
        x_copy(k).start()
    for t in range(FIRST * nk, FIRST * nk + SLOTS):
        w_copy(t, t % SLOTS).start()

    def remote(src, dst, s, r, dev):
        return pltpu.make_async_remote_copy(src_ref=src, dst_ref=dst, send_sem=s, recv_sem=r,
                                            device_id=dev, device_id_type=MESH)

    def d2d_copy(j):
        return remote(part.at[j, 1 - me_c], d2d_in.at[j], d2d_s, d2d_r.at[lax.rem(j, 4)], partner)

    def ici_copy(j):
        return remote(d2d_in.at[j, 1 - me_x], ici_in.at[j], ici_s, ici_r.at[lax.rem(j, RING)], nbr)

    def yx_copy(j):
        return remote(own.at[j], other.at[j], yx_s, yx_r.at[lax.rem(j, RING)], nbr)

    def yp_copy(j):
        return remote(own.at[j], y_out.at[j, me_c, me_x], yp_s, yp_r, partner)

    def yf_copy(j):
        return remote(other.at[j], y_out.at[j, me_c, 1 - me_x], yf_s, yf_r, partner)

    def yl_copy(j):
        return pltpu.make_async_copy(own.at[j], y_out.at[j, me_c, me_x], yl_s)

    def yo_copy(j):
        return pltpu.make_async_copy(other.at[j], y_out.at[j, me_c, 1 - me_x], yo_s)

    def stage_a(j):
        d2d_copy(j).start()

    def stage_b(j):
        d2d_copy(j).wait_recv()
        d2d_in[j, 1 - me_x] = d2d_in[j, 1 - me_x] + part[j, me_c, 1 - me_x]
        d2d_in[j, me_x] = d2d_in[j, me_x] + part[j, me_c, me_x]
        ici_copy(j).start()

    def stage_c(j):
        ici_copy(j).wait_recv()
        own[j] = (d2d_in[j, me_x] + ici_in[j]).astype(jnp.bfloat16)
        yx_copy(j).start()
        yp_copy(j).start()
        yl_copy(j).start()

    def stage_d(j):
        yx_copy(j).wait_recv()
        yf_copy(j).start()
        yo_copy(j).start()

    def when_late(j, lag, stage):
        @pl.when(j >= lag)
        def _():
            stage(j - lag)

    p_copy.wait()
    pl.semaphore_wait(barrier, 2)
    for j in range(FIRST):
        stage_a(j)
    for k in range(nk):
        x_copy(k).wait()

    @pl.loop(FIRST, nc)
    def _(j):
        for k in range(nk):
            t = j * nk + k
            slot = lax.rem(t, SLOTS)
            w_copy(t, slot).wait()
            got = jnp.dot(xc[:, k * KB:(k + 1) * KB], w_buf[slot], preferred_element_type=jnp.float32)
            for q in range(4):
                piece = got[:, q * 128:(q + 1) * 128]
                if k:
                    part[j, q // 2, q % 2] += piece
                else:
                    part[j, q // 2, q % 2] = piece

            @pl.when(t + SLOTS < total)
            def _():
                w_copy(t + SLOTS, slot).start()

            if k == 0:
                when_late(j, LAG_B, stage_b)
                when_late(j, LAG_C, stage_c)
        when_late(j, LAG_D, stage_d)
        stage_a(j)

    for step in range(nc, nc + LAG_D):
        for stage, lag in ((stage_b, LAG_B), (stage_c, LAG_C), (stage_d, LAG_D)):
            if step - lag < nc:
                stage(step - lag)

    for buf, sems in ((own, (yp_r, yf_r, yl_s, yo_s, yx_s, yp_s, yf_s)), (d2d_in, (d2d_s,)), (ici_in, (ici_s,))):
        for sem in sems:
            pltpu.make_async_copy(buf, buf, sem).wait()


def expand_kernel(len_ref, y_ref, out_hbm, buf, sem):
    tokens = out_hbm.shape[0]
    rows = y_ref.shape[3]
    seq_len = tokens // len_ref.shape[0]
    pos = lax.broadcasted_iota(jnp.int32, (tokens, rows), 1)
    place = (pos == row_targets(len_ref, (tokens, rows), 0, seq_len)).astype(jnp.bfloat16)
    steps, _, cols = buf.shape
    chunks = cols // CN

    def out_copy(i):
        return pltpu.make_async_copy(buf.at[i], out_hbm.at[:, pl.ds(i * cols, cols)], sem.at[i])

    for i in range(steps):
        wide = jnp.concatenate([y_ref[i * chunks + u, q // 2, q % 2] for u in range(chunks) for q in range(4)], axis=1)
        buf[i] = jnp.dot(place, wide, preferred_element_type=jnp.float32).astype(jnp.bfloat16)
        out_copy(i).start()
    for i in range(steps):
        out_copy(i).wait()


def solution(mesh):
    smem, hbm, vmem, anywhere = (pl.BlockSpec(memory_space=m) for m in (pltpu.SMEM, pltpu.HBM, pltpu.VMEM, pl.ANY))
    dma = lambda n: pltpu.SemaphoreType.DMA((n,))
    one = pltpu.SemaphoreType.DMA
    most = CAPS[-1]

    def with_rows(rows, xc, part, w_loc, lengths):
        depth, width = w_loc.shape
        tokens = 256
        nc, nk = width // CN, depth // KB
        y = pl.pallas_call(
            main_kernel,
            out_shape=jax.ShapeDtypeStruct((nc, 2, 2, rows, 128), jnp.bfloat16),
            in_specs=[anywhere, anywhere, hbm],
            out_specs=anywhere,
            scratch_shapes=[
                pltpu.VMEM((rows, depth), jnp.bfloat16),
                pltpu.VMEM((SLOTS, KB, CN), jnp.bfloat16),
                pltpu.VMEM((nc, 2, 2, rows, 128), jnp.float32),
                pltpu.VMEM((nc, 2, rows, 128), jnp.float32),
                pltpu.VMEM((nc, rows, 128), jnp.float32),
                pltpu.VMEM((nc, rows, 128), jnp.bfloat16),
                pltpu.VMEM((nc, rows, 128), jnp.bfloat16),
                dma(nk), one, dma(SLOTS), one, dma(4), one, dma(RING), one, dma(RING), one, one, one, one, one, one],
            compiler_params=pltpu.CompilerParams(collective_id=1 + CAPS.index(rows), has_side_effects=True, vmem_limit_bytes=44 * 2**20),
            cost_estimate=pl.CostEstimate(flops=2 * rows * depth * width, bytes_accessed=2 * depth * width, transcendentals=0),
        )(xc, part, w_loc)
        steps = nc // 2
        return pl.pallas_call(
            expand_kernel,
            out_shape=pltpu.HBM((tokens, width), jnp.bfloat16),
            in_specs=[smem, vmem],
            out_specs=hbm,
            scratch_shapes=[pltpu.VMEM((steps, tokens, width // steps), jnp.bfloat16), dma(steps)],
            compiler_params=pltpu.CompilerParams(vmem_limit_bytes=16 * 2**20),
            cost_estimate=pl.CostEstimate(flops=2 * rows * tokens * width, bytes_accessed=4 * tokens * width, transcendentals=0),
        )(lengths, y)

    def local_part(x_loc, w_loc, lengths):
        tokens, depth = x_loc.shape
        nk = depth // KB
        groups = mesh.shape["data"]
        pick, xc, part = pl.pallas_call(
            head_kernel,
            out_shape=[jax.ShapeDtypeStruct((1,), jnp.int32), jax.ShapeDtypeStruct((most, depth), jnp.bfloat16),
                       jax.ShapeDtypeStruct((FIRST, 2, 2, most, 128), jnp.float32)],
            in_specs=[smem, hbm, hbm],
            out_specs=[smem, anywhere, anywhere],
            scratch_shapes=[
                pltpu.VMEM((tokens, depth), jnp.bfloat16),
                pltpu.VMEM((most, depth), jnp.bfloat16),
                pltpu.VMEM((FIRST * nk, KB, CN), jnp.bfloat16),
                pltpu.VMEM((FIRST, 2, 2, most, 128), jnp.float32),
                pltpu.VMEM((8, 128), jnp.int32),
                pltpu.VMEM((groups - 1, 8, 128), jnp.int32),
                dma(nk), dma(FIRST * nk), dma(nk), one, dma(groups - 1), dma(groups - 1)],
            compiler_params=pltpu.CompilerParams(collective_id=0, has_side_effects=True, vmem_limit_bytes=60 * 2**20),
            cost_estimate=pl.CostEstimate(flops=2 * most * depth * CN, bytes_accessed=2 * depth * CN, transcendentals=0),
        )(lengths, x_loc, w_loc)
        return lax.switch(pick[0], [functools.partial(with_rows, cap) for cap in CAPS], xc, part, w_loc, lengths)

    return jax.shard_map(local_part, mesh=mesh, in_specs=(P("data", "tp"), P("tp", None), P("data")), out_specs=P("data", None), check_vma=False)
```

time: 83 us -> 69.8 us (0.84)
  Pallas kernels: 82.8 us -> 68.3 us
  between operations: 0.01 us -> 0.88 us
    pallas_call x2 -> x3, Pallas kernels: 82.8 us -> 68.3 us  [the longest x1 54.8 us: with_rows(): pl.pallas_call(main_kernel, out_shape=jax.ShapeDtypeStruct((nc, 2, 2, row...]
where the time goes in v2:
time: 69.8 us; the launch traced here: 69.7 us
  Pallas kernels  68.3 us (98%)
  between operations  0.88 us (1%)
    pallas_call x1, Pallas kernels, with_rows(): pl.pallas_call(main_kernel, out_shape=jax.ShapeDtypeStruct((nc, 2, 2, row...  54.8 us
    pallas_call x1, Pallas kernels, local_part(): pl.pallas_call(head_kernel, out_shape=[jax.ShapeDtypeStruct((1,), jnp.int...  10.7 us
    pallas_call x1, Pallas kernels, with_rows(): pl.pallas_call(expand_kernel, out_shape=pltpu.HBM((tokens, width), jnp.bf...  2.91 us

profile of v2, /device:TPU:0, one launch (start us, length us, event | category | flops | bytes accessed | tf_op | source)
XLA Modules:
  0.0 69.7 jit_solution(12836580624927174937)
XLA Ops:
  0.0 0.0 copy-start
  0.0 10.7 %shard_map.43 = (s32[1]{0:T(128)}, bf16[208,8192]{1,0:T(8,128)(2,1)S(1)}, f32[1,2,2,208,128]{4,3,2,1,0:T(8,128)S(1)}) custom-call(s32[4]{0:T(128)} %len_ref.1, bf16[256,8192]{1,0:T(8,128)(2,1)} %x_hbm.1, bf16[8192,8192]{1,0:T(8,128)(2,1)} %w_hbm.1), custom_call_target="tpu_custom_call" | custom-call | flops 1744830464 | bytes 8388608 | tf_op jit(solution)/shard_map/pallas_call | solution.py:295
  11.4 0.0 copy-done
  11.4 58.1 %conditional.1 = (bf16[256,8192]{1,0:T(8,128)(2,1)}) conditional(s32[]{:T(128)} %bitcast, (bf16[208,8192]{1,0:T(8,128)(2,1)S(1)}, f32[1,2,2,208,128]{4,3,2,1,0:T(8,128)S(1)}, bf16[8192,8192]{1,0:T(8,128)(2,1)}, s32[4]{0:T(128)S(1)}) %tuple.36, (bf16[208,8192]{1,0:T(8,128)(2,1)S(1)}, ...), branch_computations={%region_0.0_spmd, %region_1.0_spmd, %region_2.0_spmd, %region_3.0_... | conditional | flops 28789702656 | bytes 142606336 | solution.py:312
  11.6 54.8 %branch_3_fun.2.y_ref = bf16[16,2,2,176,128]{4,3,2,1,0:T(8,128)(2,1)S(1)} custom-call(bf16[208,8192]{1,0:T(8,128)(2,1)S(1)} %get-tuple-element.73.xc_hbm, f32[1,2,2,208,128]{4,3,2,1,0:T(8,128)S(1)} %get-tuple-element.74.part_hbm, bf16[8192,8192]{1,0:T(8,128)(2,1)} %get-tuple-element.75.w_hbm), custom_call_target="tpu_custom_call" | custom-call | flops 23622320128 | bytes 134217728 | tf_op jit(solution)/shard_map/cond/branch_3_fun/pallas_call | solution.py:263
  66.3 2.9 %branch_3_fun.3 = bf16[256,8192]{1,0:T(8,128)(2,1)} custom-call(s32[4]{0:T(128)S(1)} %get-tuple-element.72.len_ref, bf16[16,2,2,176,128]{4,3,2,1,0:T(8,128)(2,1)S(1)} %branch_3_fun.2.y_ref), custom_call_target="tpu_custom_call" | custom-call | flops 738197504 | bytes 8388608 | tf_op jit(solution)/shard_map/cond/branch_3_fun/pallas_call | solution.py:281
Async XLA Ops:
  0.0 11.4 %copy-start = (s32[4]{0:T(128)S(1)}, s32[4]{0:T(128)}, u32[]{:S(2)}) copy-start(s32[4]{0:T(128)} %len_ref.1) | copy-start | bytes 52
